TPU v7x, 256 devices: a whole 4x4x8 slice. The times are simulated.
256 devices in a mesh: section: 8 (over y, x_hi), fsdp: 32 (over x_lo, z, core).
Axes of the slice: x: 4 (x_hi: 2, x_lo: 2; x = x_hi * 2 + x_lo), y: 4, z: 8, core: 2. Of those that a mesh axis runs over, the one named last changes fastest.
Arguments:
- codes: int32 [8, 8192, 512], P('section', 'fsdp'), may hold values from 0 to 15
- scale_codes: int32 [8, 8192, 8], P('section', 'fsdp'), may hold values from 0 to 255
- second_scales: float32 [8, 256], P('section', 'fsdp'), may hold values from 0.015 to 0.09
- gains: bfloat16 [8, 8192], P('section'), may hold values from 0.5 to 1.5
- down_adapter: bfloat16 [8, 8192, 64], P('section'), may hold values from -0.0625 to 0.0625
- up_projection_weight: bfloat16 [8, 512, 64], P('section'), may hold values from -0.75 to 0.75
- hidden_in: bfloat16 [4096, 8192], P('fsdp'), may hold values from -6 to 6
- cotangent: bfloat16 [4096, 8192], P('fsdp'), may hold values from -6 to 6
Outputs:
- input_grad: bfloat16 [8, 4096, 8192], P('section', 'fsdp')
- grad_down: float32 [8, 8192, 64], P('section', 'fsdp')
- grad_up: float32 [8, 512, 64], P('section', 'fsdp')
All inputs are finite; a program needn't handle non-finite values.
Results may differ from a plain program's by a relative error of at most 0.025.
Values may be sent and summed in bfloat16 or wider, within the bound.
A program may use at most 128 MiB of HBM per device.

v0:
```python
import jax
import jax.numpy as jnp
from jax import lax
from jax.sharding import PartitionSpec as P

HEAD = 128
GROUP = 8
KV_HEADS = 4
BLOCK = 64
SROWS = 32
MICRO = 4
NF4_TABLE = (
    -1.0,
    -0.6961928009986877,
    -0.5250730514526367,
    -0.39491748809814453,
    -0.28444138169288635,
    -0.18477343022823334,
    -0.09105003625154495,
    0.0,
    0.07958029955625534,
    0.16093020141124725,
    0.24611230194568634,
    0.33791524171066284,
    0.44070982933044434,
    0.5626170039176941,
    0.7229568362236023,
    1.0,
)
adapter_scale = 0.5
epsilon = 1e-05


def from_behind(block, axis, distance):
    devices = range(lax.axis_size(axis))
    route = [(i - distance, i) for i in devices if i - distance in devices]
    return lax.ppermute(block, axis, route)


def cut_along(shard, dim, length):
    lengths = shard.shape
    tiles = shard.reshape(*lengths[:dim], length, lengths[dim] // length, *lengths[dim + 1 :])
    return jnp.moveaxis(tiles, dim, 0)


def sent_and_summed(shard, axis, dim):
    tiles = cut_along(shard, dim, lax.axis_size(axis))
    arrived = lax.all_to_all(tiles, axis, split_axis=0, concat_axis=0, tiled=True)
    return arrived.astype(jnp.float32).sum(axis=0)


def dequantize_shard(codes, scale_codes, second_scales):
    value_rows = jnp.zeros(codes.shape, jnp.float32)
    for entry in range(16):
        value_rows = jnp.where(codes == entry, jnp.float32(NF4_TABLE[entry]), value_rows)
    outer = jnp.repeat(second_scales, SROWS)
    block = outer[:, None] * (scale_codes.astype(jnp.float32) + 1.0) / 256.0
    scaled = value_rows.reshape(codes.shape[0], scale_codes.shape[1], BLOCK) * block[:, :, None]
    return scaled.reshape(codes.shape).astype(jnp.bfloat16)


def spread_heads(value_rows, width):
    count = value_rows.shape[0]
    heads = value_rows.reshape(count, KV_HEADS, 1, HEAD)
    wide = jnp.broadcast_to(heads, (count, KV_HEADS, GROUP, HEAD)).reshape(
        count, KV_HEADS * GROUP * HEAD
    )
    filler = jnp.zeros((count, width - KV_HEADS * GROUP * HEAD), value_rows.dtype)
    return jnp.concatenate([wide, filler], axis=1)


def collapse_heads(grads):
    count = grads.shape[0]
    part = grads[:, : KV_HEADS * GROUP * HEAD].reshape(count, KV_HEADS, GROUP, HEAD)
    return jnp.sum(part, axis=2).reshape(count, KV_HEADS * HEAD)


def shards(
    codes,
    scale_codes,
    second_scales,
    gains,
    down_adapter,
    up_projection_weight,
    hidden_in,
    cotangent,
):
    section = lax.axis_index("section")
    sections = lax.axis_size("section")
    shard = dequantize_shard(codes[0], scale_codes[0], second_scales[0])
    weight = lax.all_gather(shard, "fsdp", axis=0, tiled=True)
    gain = gains[0].astype(jnp.float32)
    down = down_adapter[0]
    raised_output = up_projection_weight[0]
    width = hidden_in.shape[1]
    rows = hidden_in.shape[0] // MICRO
    ticks = MICRO + sections - 1
    rank = down.shape[1]
    value_width = raised_output.shape[0]

    def forward_tick(carry, tick):
        state, saved_in, saved_normed, saved_low = carry
        incoming = from_behind(state, "section", 1)
        position = tick - section
        active = (position >= 0) & (position < MICRO)
        slot = jnp.clip(position, 0, MICRO - 1)
        first = lax.dynamic_slice_in_dim(hidden_in, slot * rows, rows, 0)
        current_in = jnp.where(section == 0, first, incoming)

        def forward_compute(operands):
            current_in, saved_in, saved_normed, saved_low = operands
            current = current_in.astype(jnp.float32)
            root_mean = jnp.sqrt(jnp.mean(current * current, axis=1, keepdims=True) + epsilon)
            normalized_input = (current / root_mean * gain).astype(jnp.bfloat16)
            narrow_product = jnp.dot(
                normalized_input, down, preferred_element_type=jnp.float32
            ).astype(jnp.bfloat16)
            value_rows = jnp.dot(
                normalized_input, weight, preferred_element_type=jnp.float32
            ) + adapter_scale * jnp.dot(
                narrow_product, raised_output.T, preferred_element_type=jnp.float32
            )
            result = (current + spread_heads(value_rows, width)).astype(jnp.bfloat16)
            return (
                result,
                lax.dynamic_update_index_in_dim(saved_in, current_in, slot, 0),
                lax.dynamic_update_index_in_dim(saved_normed, normalized_input, slot, 0),
                lax.dynamic_update_index_in_dim(saved_low, narrow_product, slot, 0),
            )

        def forward_pause(operands):
            return operands

        updated = lax.cond(
            active, forward_compute, forward_pause, (current_in, saved_in, saved_normed, saved_low)
        )
        return (updated, None)

    start = (
        jnp.zeros((rows, width), jnp.bfloat16),
        jnp.zeros((MICRO, rows, width), jnp.bfloat16),
        jnp.zeros((MICRO, rows, width), jnp.bfloat16),
        jnp.zeros((MICRO, rows, rank), jnp.bfloat16),
    )
    finished, _ = lax.scan(forward_tick, start, jnp.arange(ticks, dtype=jnp.int32))
    last_state, saved_in, saved_normed, saved_low = finished

    def backward_tick(carry, tick):
        state, saved_grad, saved_direction, saved_lowgrad = carry
        incoming = from_behind(state, "section", -1)
        position = tick - (sections - 1 - section)
        active = (position >= 0) & (position < MICRO)
        slot = jnp.clip(position, 0, MICRO - 1)
        final = lax.dynamic_slice_in_dim(cotangent, slot * rows, rows, 0)
        grad_in = jnp.where(section == sections - 1, final, incoming)

        def backward_compute(operands):
            grad_in, saved_grad, saved_direction, saved_lowgrad = operands
            current = lax.dynamic_index_in_dim(saved_in, slot, 0, keepdims=False).astype(
                jnp.float32
            )
            root_mean = jnp.sqrt(jnp.mean(current * current, axis=1, keepdims=True) + epsilon)
            unit = current / root_mean
            incoming_grad = grad_in.astype(jnp.float32)
            descent_vector = collapse_heads(incoming_grad).astype(jnp.bfloat16)
            narrow_gradient = (
                adapter_scale
                * jnp.dot(descent_vector, raised_output, preferred_element_type=jnp.float32)
            ).astype(jnp.bfloat16)
            normed_grad = jnp.dot(
                descent_vector, weight.T, preferred_element_type=jnp.float32
            ) + jnp.dot(narrow_gradient, down.T, preferred_element_type=jnp.float32)
            scaled = normed_grad * gain
            hidden_grad = (
                scaled - unit * jnp.mean(scaled * unit, axis=1, keepdims=True)
            ) / root_mean
            result = (incoming_grad + hidden_grad).astype(jnp.bfloat16)
            return (
                result,
                lax.dynamic_update_index_in_dim(saved_grad, result, slot, 0),
                lax.dynamic_update_index_in_dim(saved_direction, descent_vector, slot, 0),
                lax.dynamic_update_index_in_dim(saved_lowgrad, narrow_gradient, slot, 0),
            )

        def backward_pause(operands):
            return operands

        updated = lax.cond(
            active,
            backward_compute,
            backward_pause,
            (grad_in, saved_grad, saved_direction, saved_lowgrad),
        )
        return (updated, None)

    start_back = (
        jnp.zeros((rows, width), jnp.bfloat16),
        jnp.zeros((MICRO, rows, width), jnp.bfloat16),
        jnp.zeros((MICRO, rows, value_width), jnp.bfloat16),
        jnp.zeros((MICRO, rows, rank), jnp.bfloat16),
    )
    finished_back, _ = lax.scan(backward_tick, start_back, jnp.arange(ticks, dtype=jnp.int32))
    _, saved_grad, saved_direction, saved_lowgrad = finished_back
    tokens_here = MICRO * rows
    directions = saved_direction.reshape(tokens_here, value_width)
    lowranks = saved_low.reshape(tokens_here, rank)
    normeds = saved_normed.reshape(tokens_here, width)
    low_grads = saved_lowgrad.reshape(tokens_here, rank)
    contract = (((0,), (0,)), ((), ()))
    up_weight_gradient = adapter_scale * lax.dot_general(
        directions, lowranks, contract, preferred_element_type=jnp.float32
    )
    down_grad = lax.dot_general(normeds, low_grads, contract, preferred_element_type=jnp.float32)
    down_part, up_part = (
        sent_and_summed(down_grad.astype(jnp.bfloat16), "fsdp", 0),
        sent_and_summed(up_weight_gradient.astype(jnp.bfloat16), "fsdp", 0),
    )
    input_grad = saved_grad.reshape(1, tokens_here, width)
    return (input_grad, down_part[None], up_part[None])


def solution(mesh):
    return jax.shard_map(
        shards,
        mesh=mesh,
        in_specs=(
            P("section", "fsdp", None),
            P("section", "fsdp", None),
            P("section", "fsdp"),
            P("section", None),
            P("section", None, None),
            P("section", None, None),
            P("fsdp", None),
            P("fsdp", None),
        ),
        out_specs=(
            P("section", "fsdp", None),
            P("section", "fsdp", None),
            P("section", "fsdp", None),
        ),
        check_vma=False,
    )
```

profile of v0, /device:TPU:32, one launch (start us, length us, event | category | flops | bytes accessed | tf_op | source)
XLA Modules:
  0.0 660.1 jit_solution(1380995913632222256)
XLA Ops:
  11.6 1.8 copy.52
  13.4 90.0 %all-gather.2.cloned.1.call-done = bf16[8192,512]{0,1:T(8,128)(2,1)} async-done(((bf16[256,512]{0,1:T(8,128)(2,1)}), bf16[8192,512]{0,1:T(8,128)(2,1)}) %all-gather.2.cloned.1.call-update) | async-done | bytes 8388624 | tf_op jit(solution)/shard_map/all_gather | solution.py:91
  103.4 12.0 %copy.54 = bf16[8192,512]{1,0:T(8,128)(2,1)} copy(bf16[8192,512]{0,1:T(8,128)(2,1)} %all-gather.2.cloned.1.call-done) | data formatting | bytes 16777216 | tf_op jit(solution)/shard_map/while | solution.py:202
  115.4 1.6 broadcast.190.clone.1
  117.2 215.5 %while.35 = (s32[]{:T(128)}, bf16[32,8192]{1,0:T(8,128)(2,1)S(1)}, bf16[4,32,8192]{2,1,0:T(8,128)(2,1)S(1)}, bf16[4,32,8192]{2,1,0:T(8,128)(2,1)}, bf16[4,32,64]...) while((s32[]{:T(128)}, bf16[32,8192]{1,0:T(8,128)(2,1)S(1)}, ...), condition=%wide.region_4.5_spmd, body=%wide.region_0.4_spmd.sunk | while | flops 309102624 | bytes 25221160 | solution.py:145
  117.2 4.6 collective-permute-start
  123.0 10.3 %collective-permute-done = bf16[32,8192]{1,0:T(8,128)(2,1)S(1)} collective-permute-done((bf16[32,8192]{1,0:T(8,128)(2,1)S(1)}, bf16[32,8192]{1,0:T(8,128)(2,1)S(1)}, u32[]{:S(2)}, u32[]{:S(2)}) %collective-permute-start) | collective-permute-done | bytes 524320 | tf_op jit(solution)/shard_map/while/body/eval_jaxpr/ppermute | solution.py:37
  134.5 7.7 %conditional.4 = ((bf16[32,8192]{1,0:T(8,128)(2,1)S(1)}, bf16[4,32,8192]{2,1,0:T(8,128)(2,1)S(1)}, bf16[4,32,8192]{2,1,0:T(8,128)(2,1)}, bf16[4,32,64]{2,1,0:T(8,128)(2,1)S(1)})) conditional(s32[]{:T(128)} %convert_element_type.130, (bf16[32,8192]{1,0:T(8,128)(2,1)S(1)}, bf16[4,32,8192]{2,1,0:T(8,128)(2,1)S(1)}, bf16[4,32,8192]{2,1,0:T(8,128)(2,1)}, ...), branch_computations={%region_1.1_spmd, %region_2.3_spmd} | conditional | flops 308840480 | bytes 21550702 | solution.py:134
  134.8 5.1 fusion.6
  142.2 1.3 collective-permute-start
  144.8 9.7 %collective-permute-done = bf16[32,8192]{1,0:T(8,128)(2,1)S(1)} collective-permute-done((bf16[32,8192]{1,0:T(8,128)(2,1)S(1)}, bf16[32,8192]{1,0:T(8,128)(2,1)S(1)}, u32[]{:S(2)}, u32[]{:S(2)}) %collective-permute-start) | collective-permute-done | bytes 524320 | tf_op jit(solution)/shard_map/while/body/eval_jaxpr/ppermute | solution.py:37
  155.7 7.7 %conditional.4 = ((bf16[32,8192]{1,0:T(8,128)(2,1)S(1)}, bf16[4,32,8192]{2,1,0:T(8,128)(2,1)S(1)}, bf16[4,32,8192]{2,1,0:T(8,128)(2,1)}, bf16[4,32,64]{2,1,0:T(8,128)(2,1)S(1)})) conditional(s32[]{:T(128)} %convert_element_type.130, (bf16[32,8192]{1,0:T(8,128)(2,1)S(1)}, bf16[4,32,8192]{2,1,0:T(8,128)(2,1)S(1)}, bf16[4,32,8192]{2,1,0:T(8,128)(2,1)}, ...), branch_computations={%region_1.1_spmd, %region_2.3_spmd} | conditional | flops 308840480 | bytes 21550702 | solution.py:134
  155.9 5.1 fusion.6
  163.4 5.9 collective-permute-start
  170.6 8.8 %collective-permute-done = bf16[32,8192]{1,0:T(8,128)(2,1)S(1)} collective-permute-done((bf16[32,8192]{1,0:T(8,128)(2,1)S(1)}, bf16[32,8192]{1,0:T(8,128)(2,1)S(1)}, u32[]{:S(2)}, u32[]{:S(2)}) %collective-permute-start) | collective-permute-done | bytes 524320 | tf_op jit(solution)/shard_map/while/body/eval_jaxpr/ppermute | solution.py:37
  180.6 7.7 %conditional.4 = ((bf16[32,8192]{1,0:T(8,128)(2,1)S(1)}, bf16[4,32,8192]{2,1,0:T(8,128)(2,1)S(1)}, bf16[4,32,8192]{2,1,0:T(8,128)(2,1)}, bf16[4,32,64]{2,1,0:T(8,128)(2,1)S(1)})) conditional(s32[]{:T(128)} %convert_element_type.130, (bf16[32,8192]{1,0:T(8,128)(2,1)S(1)}, bf16[4,32,8192]{2,1,0:T(8,128)(2,1)S(1)}, bf16[4,32,8192]{2,1,0:T(8,128)(2,1)}, ...), branch_computations={%region_1.1_spmd, %region_2.3_spmd} | conditional | flops 308840480 | bytes 21550702 | solution.py:134
  180.9 5.1 fusion.6
  188.3 6.0 collective-permute-start
  195.5 8.0 %collective-permute-done = bf16[32,8192]{1,0:T(8,128)(2,1)S(1)} collective-permute-done((bf16[32,8192]{1,0:T(8,128)(2,1)S(1)}, bf16[32,8192]{1,0:T(8,128)(2,1)S(1)}, u32[]{:S(2)}, u32[]{:S(2)}) %collective-permute-start) | collective-permute-done | bytes 524320 | tf_op jit(solution)/shard_map/while/body/eval_jaxpr/ppermute | solution.py:37
  204.7 7.7 %conditional.4 = ((bf16[32,8192]{1,0:T(8,128)(2,1)S(1)}, bf16[4,32,8192]{2,1,0:T(8,128)(2,1)S(1)}, bf16[4,32,8192]{2,1,0:T(8,128)(2,1)}, bf16[4,32,64]{2,1,0:T(8,128)(2,1)S(1)})) conditional(s32[]{:T(128)} %convert_element_type.130, (bf16[32,8192]{1,0:T(8,128)(2,1)S(1)}, bf16[4,32,8192]{2,1,0:T(8,128)(2,1)S(1)}, bf16[4,32,8192]{2,1,0:T(8,128)(2,1)}, ...), branch_computations={%region_1.1_spmd, %region_2.3_spmd} | conditional | flops 308840480 | bytes 21550702 | solution.py:134
  204.9 5.1 fusion.6
  212.3 5.9 collective-permute-start
  219.5 7.1 %collective-permute-done = bf16[32,8192]{1,0:T(8,128)(2,1)S(1)} collective-permute-done((bf16[32,8192]{1,0:T(8,128)(2,1)S(1)}, bf16[32,8192]{1,0:T(8,128)(2,1)S(1)}, u32[]{:S(2)}, u32[]{:S(2)}) %collective-permute-start) | collective-permute-done | bytes 524320 | tf_op jit(solution)/shard_map/while/body/eval_jaxpr/ppermute | solution.py:37
  227.9 13.6 %collective-permute-start = (bf16[32,8192]{1,0:T(8,128)(2,1)S(1)}, bf16[32,8192]{1,0:T(8,128)(2,1)S(1)}, u32[]{:S(2)}, u32[]{:S(2)}) collective-permute-start(bf16[32,8192]{1,0:T(8,128)(2,1)S(1)} %get-tuple-element.701), channel_id=1, source_target_pairs={{0,32},{32,64},{64,96},{96,128},{128,160},{160,192},{192,224},{1,3... | collective-permute-start | bytes 1572872 | tf_op jit(solution)/shard_map/while/body/eval_jaxpr/ppermute | solution.py:37
  242.7 6.3 collective-permute-done
  250.2 5.9 collective-permute-start
  257.3 5.6 collective-permute-done
  264.2 14.5 %collective-permute-start = (bf16[32,8192]{1,0:T(8,128)(2,1)S(1)}, bf16[32,8192]{1,0:T(8,128)(2,1)S(1)}, u32[]{:S(2)}, u32[]{:S(2)}) collective-permute-start(bf16[32,8192]{1,0:T(8,128)(2,1)S(1)} %get-tuple-element.701), channel_id=1, source_target_pairs={{0,32},{32,64},{64,96},{96,128},{128,160},{160,192},{192,224},{1,3... | collective-permute-start | bytes 1572872 | tf_op jit(solution)/shard_map/while/body/eval_jaxpr/ppermute | solution.py:37
  279.9 5.4 collective-permute-done
  286.5 6.8 %collective-permute-start = (bf16[32,8192]{1,0:T(8,128)(2,1)S(1)}, bf16[32,8192]{1,0:T(8,128)(2,1)S(1)}, u32[]{:S(2)}, u32[]{:S(2)}) collective-permute-start(bf16[32,8192]{1,0:T(8,128)(2,1)S(1)} %get-tuple-element.701), channel_id=1, source_target_pairs={{0,32},{32,64},{64,96},{96,128},{128,160},{160,192},{192,224},{1,3... | collective-permute-start | bytes 1572872 | tf_op jit(solution)/shard_map/while/body/eval_jaxpr/ppermute | solution.py:37
  294.6 5.4 collective-permute-done
  301.2 9.0 %collective-permute-start = (bf16[32,8192]{1,0:T(8,128)(2,1)S(1)}, bf16[32,8192]{1,0:T(8,128)(2,1)S(1)}, u32[]{:S(2)}, u32[]{:S(2)}) collective-permute-start(bf16[32,8192]{1,0:T(8,128)(2,1)S(1)} %get-tuple-element.701), channel_id=1, source_target_pairs={{0,32},{32,64},{64,96},{96,128},{128,160},{160,192},{192,224},{1,3... | collective-permute-start | bytes 1572872 | tf_op jit(solution)/shard_map/while/body/eval_jaxpr/ppermute | solution.py:37
  311.4 5.4 collective-permute-done
  318.0 6.8 %collective-permute-start = (bf16[32,8192]{1,0:T(8,128)(2,1)S(1)}, bf16[32,8192]{1,0:T(8,128)(2,1)S(1)}, u32[]{:S(2)}, u32[]{:S(2)}) collective-permute-start(bf16[32,8192]{1,0:T(8,128)(2,1)S(1)} %get-tuple-element.701), channel_id=1, source_target_pairs={{0,32},{32,64},{64,96},{96,128},{128,160},{160,192},{192,224},{1,3... | collective-permute-start | bytes 1572872 | tf_op jit(solution)/shard_map/while/body/eval_jaxpr/ppermute | solution.py:37
  326.1 5.4 collective-permute-done
  332.8 1.5 broadcast.190
  334.3 271.0 %while.36 = (s32[]{:T(128)}, bf16[32,8192]{1,0:T(8,128)(2,1)S(1)}, bf16[4,32,8192]{2,1,0:T(8,128)(2,1)}, bf16[4,32,512]{2,1,0:T(8,128)(2,1)S(1)}, bf16[4,32,64]{...) while((s32[]{:T(128)}, bf16[32,8192]{1,0:T(8,128)(2,1)S(1)}, ...), condition=%wide.region_11.12_spmd, body=%wide.region_5.11_spmd.sunk | while | flops 309186592 | bytes 28268232 | solution.py:202
  336.8 19.6 %collective-permute-done.1 = bf16[32,8192]{1,0:T(8,128)(2,1)S(1)} collective-permute-done((bf16[32,8192]{1,0:T(8,128)(2,1)S(1)}, bf16[32,8192]{1,0:T(8,128)(2,1)S(1)}, u32[]{:S(2)}, u32[]{:S(2)}) %collective-permute-start.1) | collective-permute-done | bytes 524320 | tf_op jit(solution)/shard_map/while/body/eval_jaxpr/ppermute | solution.py:37
  357.6 1.3 collective-permute-start.1
  360.2 11.3 %collective-permute-done.1 = bf16[32,8192]{1,0:T(8,128)(2,1)S(1)} collective-permute-done((bf16[32,8192]{1,0:T(8,128)(2,1)S(1)}, bf16[32,8192]{1,0:T(8,128)(2,1)S(1)}, u32[]{:S(2)}, u32[]{:S(2)}) %collective-permute-start.1) | collective-permute-done | bytes 524320 | tf_op jit(solution)/shard_map/while/body/eval_jaxpr/ppermute | solution.py:37
  372.7 1.3 collective-permute-start.1
  375.3 22.6 %collective-permute-done.1 = bf16[32,8192]{1,0:T(8,128)(2,1)S(1)} collective-permute-done((bf16[32,8192]{1,0:T(8,128)(2,1)S(1)}, bf16[32,8192]{1,0:T(8,128)(2,1)S(1)}, u32[]{:S(2)}, u32[]{:S(2)}) %collective-permute-start.1) | collective-permute-done | bytes 524320 | tf_op jit(solution)/shard_map/while/body/eval_jaxpr/ppermute | solution.py:37
  399.0 1.3 collective-permute-start.1
  401.6 14.8 %collective-permute-done.1 = bf16[32,8192]{1,0:T(8,128)(2,1)S(1)} collective-permute-done((bf16[32,8192]{1,0:T(8,128)(2,1)S(1)}, bf16[32,8192]{1,0:T(8,128)(2,1)S(1)}, u32[]{:S(2)}, u32[]{:S(2)}) %collective-permute-start.1) | collective-permute-done | bytes 524320 | tf_op jit(solution)/shard_map/while/body/eval_jaxpr/ppermute | solution.py:37
  420.1 19.9 %collective-permute-done.1 = bf16[32,8192]{1,0:T(8,128)(2,1)S(1)} collective-permute-done((bf16[32,8192]{1,0:T(8,128)(2,1)S(1)}, bf16[32,8192]{1,0:T(8,128)(2,1)S(1)}, u32[]{:S(2)}, u32[]{:S(2)}) %collective-permute-start.1) | collective-permute-done | bytes 524320 | tf_op jit(solution)/shard_map/while/body/eval_jaxpr/ppermute | solution.py:37
  443.8 17.1 %collective-permute-done.1 = bf16[32,8192]{1,0:T(8,128)(2,1)S(1)} collective-permute-done((bf16[32,8192]{1,0:T(8,128)(2,1)S(1)}, bf16[32,8192]{1,0:T(8,128)(2,1)S(1)}, u32[]{:S(2)}, u32[]{:S(2)}) %collective-permute-start.1) | collective-permute-done | bytes 524320 | tf_op jit(solution)/shard_map/while/body/eval_jaxpr/ppermute | solution.py:37
  464.7 10.0 %collective-permute-done.1 = bf16[32,8192]{1,0:T(8,128)(2,1)S(1)} collective-permute-done((bf16[32,8192]{1,0:T(8,128)(2,1)S(1)}, bf16[32,8192]{1,0:T(8,128)(2,1)S(1)}, u32[]{:S(2)}, u32[]{:S(2)}) %collective-permute-start.1) | collective-permute-done | bytes 524320 | tf_op jit(solution)/shard_map/while/body/eval_jaxpr/ppermute | solution.py:37
  478.5 43.8 %collective-permute-done.1 = bf16[32,8192]{1,0:T(8,128)(2,1)S(1)} collective-permute-done((bf16[32,8192]{1,0:T(8,128)(2,1)S(1)}, bf16[32,8192]{1,0:T(8,128)(2,1)S(1)}, u32[]{:S(2)}, u32[]{:S(2)}) %collective-permute-start.1) | collective-permute-done | bytes 524320 | tf_op jit(solution)/shard_map/while/body/eval_jaxpr/ppermute | solution.py:37
  523.5 8.8 %conditional.5 = ((bf16[32,8192]{1,0:T(8,128)(2,1)S(1)}, bf16[4,32,8192]{2,1,0:T(8,128)(2,1)}, bf16[4,32,512]{2,1,0:T(8,128)(2,1)S(1)}, bf16[4,32,64]{2,1,0:T(8,128)(2,1)S(1)})) conditional(s32[]{:T(128)} %convert_element_type.131, (bf16[32,8192]{1,0:T(8,128)(2,1)S(1)}, bf16[4,32,8192]{2,1,0:T(8,128)(2,1)}, bf16[4,32,512]{2,1,0:T(8,128)(2,1)S(1)}, ...), branch_computations={%region_6.6_spmd, %region_7.10_spmd} | conditional | flops 308924448 | bytes 24597758 | solution.py:188
  523.9 6.1 fusion.12
  534.9 10.9 %collective-permute-done.1 = bf16[32,8192]{1,0:T(8,128)(2,1)S(1)} collective-permute-done((bf16[32,8192]{1,0:T(8,128)(2,1)S(1)}, bf16[32,8192]{1,0:T(8,128)(2,1)S(1)}, u32[]{:S(2)}, u32[]{:S(2)}) %collective-permute-start.1) | collective-permute-done | bytes 524320 | tf_op jit(solution)/shard_map/while/body/eval_jaxpr/ppermute | solution.py:37
  547.0 8.8 %conditional.5 = ((bf16[32,8192]{1,0:T(8,128)(2,1)S(1)}, bf16[4,32,8192]{2,1,0:T(8,128)(2,1)}, bf16[4,32,512]{2,1,0:T(8,128)(2,1)S(1)}, bf16[4,32,64]{2,1,0:T(8,128)(2,1)S(1)})) conditional(s32[]{:T(128)} %convert_element_type.131, (bf16[32,8192]{1,0:T(8,128)(2,1)S(1)}, bf16[4,32,8192]{2,1,0:T(8,128)(2,1)}, bf16[4,32,512]{2,1,0:T(8,128)(2,1)S(1)}, ...), branch_computations={%region_6.6_spmd, %region_7.10_spmd} | conditional | flops 308924448 | bytes 24597758 | solution.py:188
  547.4 6.1 fusion.12
  558.3 11.5 %collective-permute-done.1 = bf16[32,8192]{1,0:T(8,128)(2,1)S(1)} collective-permute-done((bf16[32,8192]{1,0:T(8,128)(2,1)S(1)}, bf16[32,8192]{1,0:T(8,128)(2,1)S(1)}, u32[]{:S(2)}, u32[]{:S(2)}) %collective-permute-start.1) | collective-permute-done | bytes 524320 | tf_op jit(solution)/shard_map/while/body/eval_jaxpr/ppermute | solution.py:37
  571.0 8.8 %conditional.5 = ((bf16[32,8192]{1,0:T(8,128)(2,1)S(1)}, bf16[4,32,8192]{2,1,0:T(8,128)(2,1)}, bf16[4,32,512]{2,1,0:T(8,128)(2,1)S(1)}, bf16[4,32,64]{2,1,0:T(8,128)(2,1)S(1)})) conditional(s32[]{:T(128)} %convert_element_type.131, (bf16[32,8192]{1,0:T(8,128)(2,1)S(1)}, bf16[4,32,8192]{2,1,0:T(8,128)(2,1)}, bf16[4,32,512]{2,1,0:T(8,128)(2,1)S(1)}, ...), branch_computations={%region_6.6_spmd, %region_7.10_spmd} | conditional | flops 308924448 | bytes 24597758 | solution.py:188
  571.4 6.1 fusion.12
  582.4 12.9 %collective-permute-done.1 = bf16[32,8192]{1,0:T(8,128)(2,1)S(1)} collective-permute-done((bf16[32,8192]{1,0:T(8,128)(2,1)S(1)}, bf16[32,8192]{1,0:T(8,128)(2,1)S(1)}, u32[]{:S(2)}, u32[]{:S(2)}) %collective-permute-start.1) | collective-permute-done | bytes 524320 | tf_op jit(solution)/shard_map/while/body/eval_jaxpr/ppermute | solution.py:37
  596.4 8.8 %conditional.5 = ((bf16[32,8192]{1,0:T(8,128)(2,1)S(1)}, bf16[4,32,8192]{2,1,0:T(8,128)(2,1)}, bf16[4,32,512]{2,1,0:T(8,128)(2,1)S(1)}, bf16[4,32,64]{2,1,0:T(8,128)(2,1)S(1)})) conditional(s32[]{:T(128)} %convert_element_type.131, (bf16[32,8192]{1,0:T(8,128)(2,1)S(1)}, bf16[4,32,8192]{2,1,0:T(8,128)(2,1)}, bf16[4,32,512]{2,1,0:T(8,128)(2,1)S(1)}, ...), branch_computations={%region_6.6_spmd, %region_7.10_spmd} | conditional | flops 308924448 | bytes 24597758 | solution.py:188
  596.9 6.1 fusion.12
  606.4 4.2 all-to-all-start.1
  610.5 2.1 fusion.16
  613.7 4.7 all-to-all-done.1
  618.4 5.0 all-to-all-start
  624.2 28.3 %all-to-all-done = bf16[32,256,64]{1,2,0:T(8,128)(2,1)S(1)} async-done(((bf16[32,256,64]{1,2,0:T(8,128)(2,1)}), bf16[32,256,64]{1,2,0:T(8,128)(2,1)S(1)}, u32[]{:S(2)}, u32[]{:S(2)}) %all-to-all-start) | async-done | bytes 1048608 | tf_op jit(solution)/shard_map/all_to_all | solution.py:48
  (196 shorter events, 78.1 us)
Async XLA Ops:
  7.2 4.2 copy-start.4
  7.2 4.3 copy-start.3
  7.2 4.4 copy-start.2
  7.2 96.2 %all-gather.2.cloned.1.call-start = ((), (), s32[]{:S(2)}) async-start(), calls=%async_computation.2 | async-start | bytes 8650752 | tf_op jit(solution)/shard_map/all_gather | solution.py:91
  117.2 16.1 %collective-permute-start = (bf16[32,8192]{1,0:T(8,128)(2,1)S(1)}, bf16[32,8192]{1,0:T(8,128)(2,1)S(1)}, u32[]{:S(2)}, u32[]{:S(2)}) collective-permute-start(bf16[32,8192]{1,0:T(8,128)(2,1)S(1)} %get-tuple-element.701), channel_id=1, source_target_pairs={{0,32},{32,64},{64,96},{96,128},{128,160},{160,192},{192,224},{1,3... | collective-permute-start | bytes 1572872 | tf_op jit(solution)/shard_map/while/body/eval_jaxpr/ppermute | solution.py:37
  134.7 5.1 copy-start
  142.2 12.3 %collective-permute-start = (bf16[32,8192]{1,0:T(8,128)(2,1)S(1)}, bf16[32,8192]{1,0:T(8,128)(2,1)S(1)}, u32[]{:S(2)}, u32[]{:S(2)}) collective-permute-start(bf16[32,8192]{1,0:T(8,128)(2,1)S(1)} %get-tuple-element.701), channel_id=1, source_target_pairs={{0,32},{32,64},{64,96},{96,128},{128,160},{160,192},{192,224},{1,3... | collective-permute-start | bytes 1572872 | tf_op jit(solution)/shard_map/while/body/eval_jaxpr/ppermute | solution.py:37
  155.9 5.1 copy-start
  163.4 16.0 %collective-permute-start = (bf16[32,8192]{1,0:T(8,128)(2,1)S(1)}, bf16[32,8192]{1,0:T(8,128)(2,1)S(1)}, u32[]{:S(2)}, u32[]{:S(2)}) collective-permute-start(bf16[32,8192]{1,0:T(8,128)(2,1)S(1)} %get-tuple-element.701), channel_id=1, source_target_pairs={{0,32},{32,64},{64,96},{96,128},{128,160},{160,192},{192,224},{1,3... | collective-permute-start | bytes 1572872 | tf_op jit(solution)/shard_map/while/body/eval_jaxpr/ppermute | solution.py:37
  180.9 5.1 copy-start
  188.3 15.2 %collective-permute-start = (bf16[32,8192]{1,0:T(8,128)(2,1)S(1)}, bf16[32,8192]{1,0:T(8,128)(2,1)S(1)}, u32[]{:S(2)}, u32[]{:S(2)}) collective-permute-start(bf16[32,8192]{1,0:T(8,128)(2,1)S(1)} %get-tuple-element.701), channel_id=1, source_target_pairs={{0,32},{32,64},{64,96},{96,128},{128,160},{160,192},{192,224},{1,3... | collective-permute-start | bytes 1572872 | tf_op jit(solution)/shard_map/while/body/eval_jaxpr/ppermute | solution.py:37
  204.9 5.1 copy-start
  212.3 14.3 %collective-permute-start = (bf16[32,8192]{1,0:T(8,128)(2,1)S(1)}, bf16[32,8192]{1,0:T(8,128)(2,1)S(1)}, u32[]{:S(2)}, u32[]{:S(2)}) collective-permute-start(bf16[32,8192]{1,0:T(8,128)(2,1)S(1)} %get-tuple-element.701), channel_id=1, source_target_pairs={{0,32},{32,64},{64,96},{96,128},{128,160},{160,192},{192,224},{1,3... | collective-permute-start | bytes 1572872 | tf_op jit(solution)/shard_map/while/body/eval_jaxpr/ppermute | solution.py:37
  227.9 21.1 %collective-permute-start = (bf16[32,8192]{1,0:T(8,128)(2,1)S(1)}, bf16[32,8192]{1,0:T(8,128)(2,1)S(1)}, u32[]{:S(2)}, u32[]{:S(2)}) collective-permute-start(bf16[32,8192]{1,0:T(8,128)(2,1)S(1)} %get-tuple-element.701), channel_id=1, source_target_pairs={{0,32},{32,64},{64,96},{96,128},{128,160},{160,192},{192,224},{1,3... | collective-permute-start | bytes 1572872 | tf_op jit(solution)/shard_map/while/body/eval_jaxpr/ppermute | solution.py:37
  250.2 12.8 %collective-permute-start = (bf16[32,8192]{1,0:T(8,128)(2,1)S(1)}, bf16[32,8192]{1,0:T(8,128)(2,1)S(1)}, u32[]{:S(2)}, u32[]{:S(2)}) collective-permute-start(bf16[32,8192]{1,0:T(8,128)(2,1)S(1)} %get-tuple-element.701), channel_id=1, source_target_pairs={{0,32},{32,64},{64,96},{96,128},{128,160},{160,192},{192,224},{1,3... | collective-permute-start | bytes 1572872 | tf_op jit(solution)/shard_map/while/body/eval_jaxpr/ppermute | solution.py:37
  264.2 21.1 %collective-permute-start = (bf16[32,8192]{1,0:T(8,128)(2,1)S(1)}, bf16[32,8192]{1,0:T(8,128)(2,1)S(1)}, u32[]{:S(2)}, u32[]{:S(2)}) collective-permute-start(bf16[32,8192]{1,0:T(8,128)(2,1)S(1)} %get-tuple-element.701), channel_id=1, source_target_pairs={{0,32},{32,64},{64,96},{96,128},{128,160},{160,192},{192,224},{1,3... | collective-permute-start | bytes 1572872 | tf_op jit(solution)/shard_map/while/body/eval_jaxpr/ppermute | solution.py:37
  286.5 13.5 %collective-permute-start = (bf16[32,8192]{1,0:T(8,128)(2,1)S(1)}, bf16[32,8192]{1,0:T(8,128)(2,1)S(1)}, u32[]{:S(2)}, u32[]{:S(2)}) collective-permute-start(bf16[32,8192]{1,0:T(8,128)(2,1)S(1)} %get-tuple-element.701), channel_id=1, source_target_pairs={{0,32},{32,64},{64,96},{96,128},{128,160},{160,192},{192,224},{1,3... | collective-permute-start | bytes 1572872 | tf_op jit(solution)/shard_map/while/body/eval_jaxpr/ppermute | solution.py:37
  301.2 15.6 %collective-permute-start = (bf16[32,8192]{1,0:T(8,128)(2,1)S(1)}, bf16[32,8192]{1,0:T(8,128)(2,1)S(1)}, u32[]{:S(2)}, u32[]{:S(2)}) collective-permute-start(bf16[32,8192]{1,0:T(8,128)(2,1)S(1)} %get-tuple-element.701), channel_id=1, source_target_pairs={{0,32},{32,64},{64,96},{96,128},{128,160},{160,192},{192,224},{1,3... | collective-permute-start | bytes 1572872 | tf_op jit(solution)/shard_map/while/body/eval_jaxpr/ppermute | solution.py:37
  318.0 13.5 %collective-permute-start = (bf16[32,8192]{1,0:T(8,128)(2,1)S(1)}, bf16[32,8192]{1,0:T(8,128)(2,1)S(1)}, u32[]{:S(2)}, u32[]{:S(2)}) collective-permute-start(bf16[32,8192]{1,0:T(8,128)(2,1)S(1)} %get-tuple-element.701), channel_id=1, source_target_pairs={{0,32},{32,64},{64,96},{96,128},{128,160},{160,192},{192,224},{1,3... | collective-permute-start | bytes 1572872 | tf_op jit(solution)/shard_map/while/body/eval_jaxpr/ppermute | solution.py:37
  334.3 22.1 %collective-permute-start.1 = (bf16[32,8192]{1,0:T(8,128)(2,1)S(1)}, bf16[32,8192]{1,0:T(8,128)(2,1)S(1)}, u32[]{:S(2)}, u32[]{:S(2)}) collective-permute-start(bf16[32,8192]{1,0:T(8,128)(2,1)S(1)} %get-tuple-element.759), channel_id=1, source_target_pairs={{32,0},{64,32},{96,64},{128,96},{160,128},{192,160},{224,192},{33,... | collective-permute-start | bytes 1572872 | tf_op jit(solution)/shard_map/while/body/eval_jaxpr/ppermute | solution.py:37
  357.6 13.9 %collective-permute-start.1 = (bf16[32,8192]{1,0:T(8,128)(2,1)S(1)}, bf16[32,8192]{1,0:T(8,128)(2,1)S(1)}, u32[]{:S(2)}, u32[]{:S(2)}) collective-permute-start(bf16[32,8192]{1,0:T(8,128)(2,1)S(1)} %get-tuple-element.759), channel_id=1, source_target_pairs={{32,0},{64,32},{96,64},{128,96},{160,128},{192,160},{224,192},{33,... | collective-permute-start | bytes 1572872 | tf_op jit(solution)/shard_map/while/body/eval_jaxpr/ppermute | solution.py:37
  372.7 25.1 %collective-permute-start.1 = (bf16[32,8192]{1,0:T(8,128)(2,1)S(1)}, bf16[32,8192]{1,0:T(8,128)(2,1)S(1)}, u32[]{:S(2)}, u32[]{:S(2)}) collective-permute-start(bf16[32,8192]{1,0:T(8,128)(2,1)S(1)} %get-tuple-element.759), channel_id=1, source_target_pairs={{32,0},{64,32},{96,64},{128,96},{160,128},{192,160},{224,192},{33,... | collective-permute-start | bytes 1572872 | tf_op jit(solution)/shard_map/while/body/eval_jaxpr/ppermute | solution.py:37
  399.0 17.3 %collective-permute-start.1 = (bf16[32,8192]{1,0:T(8,128)(2,1)S(1)}, bf16[32,8192]{1,0:T(8,128)(2,1)S(1)}, u32[]{:S(2)}, u32[]{:S(2)}) collective-permute-start(bf16[32,8192]{1,0:T(8,128)(2,1)S(1)} %get-tuple-element.759), channel_id=1, source_target_pairs={{32,0},{64,32},{96,64},{128,96},{160,128},{192,160},{224,192},{33,... | collective-permute-start | bytes 1572872 | tf_op jit(solution)/shard_map/while/body/eval_jaxpr/ppermute | solution.py:37
  417.6 22.5 %collective-permute-start.1 = (bf16[32,8192]{1,0:T(8,128)(2,1)S(1)}, bf16[32,8192]{1,0:T(8,128)(2,1)S(1)}, u32[]{:S(2)}, u32[]{:S(2)}) collective-permute-start(bf16[32,8192]{1,0:T(8,128)(2,1)S(1)} %get-tuple-element.759), channel_id=1, source_target_pairs={{32,0},{64,32},{96,64},{128,96},{160,128},{192,160},{224,192},{33,... | collective-permute-start | bytes 1572872 | tf_op jit(solution)/shard_map/while/body/eval_jaxpr/ppermute | solution.py:37
  441.3 19.6 %collective-permute-start.1 = (bf16[32,8192]{1,0:T(8,128)(2,1)S(1)}, bf16[32,8192]{1,0:T(8,128)(2,1)S(1)}, u32[]{:S(2)}, u32[]{:S(2)}) collective-permute-start(bf16[32,8192]{1,0:T(8,128)(2,1)S(1)} %get-tuple-element.759), channel_id=1, source_target_pairs={{32,0},{64,32},{96,64},{128,96},{160,128},{192,160},{224,192},{33,... | collective-permute-start | bytes 1572872 | tf_op jit(solution)/shard_map/while/body/eval_jaxpr/ppermute | solution.py:37
  462.1 12.6 %collective-permute-start.1 = (bf16[32,8192]{1,0:T(8,128)(2,1)S(1)}, bf16[32,8192]{1,0:T(8,128)(2,1)S(1)}, u32[]{:S(2)}, u32[]{:S(2)}) collective-permute-start(bf16[32,8192]{1,0:T(8,128)(2,1)S(1)} %get-tuple-element.759), channel_id=1, source_target_pairs={{32,0},{64,32},{96,64},{128,96},{160,128},{192,160},{224,192},{33,... | collective-permute-start | bytes 1572872 | tf_op jit(solution)/shard_map/while/body/eval_jaxpr/ppermute | solution.py:37
  475.9 46.4 %collective-permute-start.1 = (bf16[32,8192]{1,0:T(8,128)(2,1)S(1)}, bf16[32,8192]{1,0:T(8,128)(2,1)S(1)}, u32[]{:S(2)}, u32[]{:S(2)}) collective-permute-start(bf16[32,8192]{1,0:T(8,128)(2,1)S(1)} %get-tuple-element.759), channel_id=1, source_target_pairs={{32,0},{64,32},{96,64},{128,96},{160,128},{192,160},{224,192},{33,... | collective-permute-start | bytes 1572872 | tf_op jit(solution)/shard_map/while/body/eval_jaxpr/ppermute | solution.py:37
  523.9 6.2 copy-start.1
  532.3 13.5 %collective-permute-start.1 = (bf16[32,8192]{1,0:T(8,128)(2,1)S(1)}, bf16[32,8192]{1,0:T(8,128)(2,1)S(1)}, u32[]{:S(2)}, u32[]{:S(2)}) collective-permute-start(bf16[32,8192]{1,0:T(8,128)(2,1)S(1)} %get-tuple-element.759), channel_id=1, source_target_pairs={{32,0},{64,32},{96,64},{128,96},{160,128},{192,160},{224,192},{33,... | collective-permute-start | bytes 1572872 | tf_op jit(solution)/shard_map/while/body/eval_jaxpr/ppermute | solution.py:37
  547.4 6.2 copy-start.1
  555.8 14.0 %collective-permute-start.1 = (bf16[32,8192]{1,0:T(8,128)(2,1)S(1)}, bf16[32,8192]{1,0:T(8,128)(2,1)S(1)}, u32[]{:S(2)}, u32[]{:S(2)}) collective-permute-start(bf16[32,8192]{1,0:T(8,128)(2,1)S(1)} %get-tuple-element.759), channel_id=1, source_target_pairs={{32,0},{64,32},{96,64},{128,96},{160,128},{192,160},{224,192},{33,... | collective-permute-start | bytes 1572872 | tf_op jit(solution)/shard_map/while/body/eval_jaxpr/ppermute | solution.py:37
  571.4 6.2 copy-start.1
  579.8 15.5 %collective-permute-start.1 = (bf16[32,8192]{1,0:T(8,128)(2,1)S(1)}, bf16[32,8192]{1,0:T(8,128)(2,1)S(1)}, u32[]{:S(2)}, u32[]{:S(2)}) collective-permute-start(bf16[32,8192]{1,0:T(8,128)(2,1)S(1)} %get-tuple-element.759), channel_id=1, source_target_pairs={{32,0},{64,32},{96,64},{128,96},{160,128},{192,160},{224,192},{33,... | collective-permute-start | bytes 1572872 | tf_op jit(solution)/shard_map/while/body/eval_jaxpr/ppermute | solution.py:37
  596.9 6.2 copy-start.1
  606.4 12.1 %all-to-all-start.1 = ((bf16[32,2,512]{2,1,0:T(2,128)(2,1)}), bf16[32,2,512]{2,1,0:T(2,128)(2,1)S(1)}, u32[]{:S(2)}, u32[]{:S(2)}) async-start(bf16[32,2,512]{2,1,0:T(2,128)(2,1)} %reshape.170), calls=%async_computation.1 | async-start | bytes 131072 | tf_op jit(solution)/shard_map/all_to_all | solution.py:48
  618.4 34.1 %all-to-all-start = ((bf16[32,256,64]{1,2,0:T(8,128)(2,1)}), bf16[32,256,64]{1,2,0:T(8,128)(2,1)S(1)}, u32[]{:S(2)}, u32[]{:S(2)}) async-start(bf16[32,256,64]{1,2,0:T(8,128)(2,1)} %bitcast.84), calls=%async_computation | async-start | bytes 2097152 | tf_op jit(solution)/shard_map/all_to_all | solution.py:48
Sparse Core Ops, SparseCore 0:
  11.5 91.8 all-gather.1
where the time goes:
time: 663 us; the launch traced here: 660 us
  waiting for transfers between devices  395 us (60%)
  starting transfers between devices  104 us (16%)
  matrix products  54 us (8%)
  other arithmetic  40.8 us (6%)
  local copies, waits for them, and re-layouts  36.4 us (5%)
  loops' own time  16.3 us (2%)
  between operations  14.2 us (2%)
    ppermute x22, waiting for transfers between devices, from_behind(): return lax.ppermute(block, axis, route)  272 us
    ppermute x22, starting transfers between devices, from_behind(): return lax.ppermute(block, axis, route)  94.5 us
    all_gather x1, waiting for transfers between devices, shards(): weight = lax.all_gather(shard, 'fsdp', axis=0, tiled=True)  90 us
    all_to_all x2, waiting for transfers between devices, sent_and_summed(): lax.all_to_all(tiles, axis, split_axis=0, concat_axis=0, tiled=True)  33 us
    dot_general x4, matrix products, backward_compute(): jnp.dot(descent_vector, weight.T, preferred_element_type=jnp.float32)  24.2 us
    dot_general x4, matrix products, forward_compute(): jnp.dot(normalized_input, weight, preferred_element_type=jnp.float32)  20.5 us
  transfers between devices with their start and end apart: 25, of which 25 were waited for; matrix products, arithmetic and copies ran while one was open for 3% of the time, Pallas kernels for 0%

commit v1 on v0

--- a/solution.py
+++ b/solution.py
@@ -88,7 +88,9 @@
     section = lax.axis_index("section")
     sections = lax.axis_size("section")
     shard = dequantize_shard(codes[0], scale_codes[0], second_scales[0])
-    weight = lax.all_gather(shard, "fsdp", axis=0, tiled=True)
+    weight = jnp.concatenate(
+        lax.all_to_all(jnp.stack([shard] * lax.axis_size("fsdp"), axis=0), "fsdp", 0, 0), axis=0
+    )
     gain = gains[0].astype(jnp.float32)
     down = down_adapter[0]
     raised_output = up_projection_weight[0]

time: 663 us -> 761 us (1.15)
  waiting for transfers between devices: 395 us -> 488 us
  starting transfers between devices: 104 us -> 124 us
  between operations: 14.2 us -> 0.81 us
    all_to_all x0 -> x1, waiting for transfers between devices: none -> 181 us  [shards(): lax.all_to_all(jnp.stack([shard] * lax.axis_size('fsdp'), axis=0), 'fsdp'...]
    all_gather x1 -> x0, waiting for transfers between devices: 90 us -> none  [shards(): weight = lax.all_gather(shard, 'fsdp', axis=0, tiled=True)]
    while x1 -> x0, local copies, waits for them, and re-layouts: 12 us -> none  [shards(): lax.scan(backward_tick, start_back, jnp.arange(ticks, dtype=jnp.int32))]
    all_to_all x0 -> x1, starting transfers between devices: none -> 9.84 us  [shards(): lax.all_to_all(jnp.stack([shard] * lax.axis_size('fsdp'), axis=0), 'fsdp'...]
where the time goes in v1:
time: 761 us; the launch traced here: 759 us
  waiting for transfers between devices  488 us (64%)
  starting transfers between devices  124 us (16%)
  matrix products  59.7 us (8%)
  other arithmetic  40 us (5%)
  local copies, waits for them, and re-layouts  29.5 us (4%)
  loops' own time  16.7 us (2%)
    ppermute x22, waiting for transfers between devices, from_behind(): return lax.ppermute(block, axis, route)  274 us
    all_to_all x1, waiting for transfers between devices, shards(): lax.all_to_all(jnp.stack([shard] * lax.axis_size('fsdp'), axis=0), 'fsdp'...  181 us
    ppermute x22, starting transfers between devices, from_behind(): return lax.ppermute(block, axis, route)  99.5 us
    all_to_all x2, waiting for transfers between devices, sent_and_summed(): lax.all_to_all(tiles, axis, split_axis=0, concat_axis=0, tiled=True)  33.1 us
    dot_general x4, matrix products, backward_compute(): jnp.dot(descent_vector, weight.T, preferred_element_type=jnp.float32)  24.2 us
    dot_general x4, matrix products, forward_compute(): jnp.dot(normalized_input, weight, preferred_element_type=jnp.float32)  19.9 us
  transfers between devices with their start and end apart: 25, of which 25 were waited for; matrix products, arithmetic and copies ran while one was open for 3% of the time, Pallas kernels for 0%

profile of v1, /device:TPU:32, one launch (start us, length us, event | category | flops | bytes accessed | tf_op | source)
XLA Modules:
  0.0 758.7 jit_solution(12123168122989946652)
XLA Ops:
  4.1 4.2 stack.5
  8.3 9.8 %all-to-all-start = ((bf16[32,256,512]{2,1,0:T(8,128)(2,1)}), bf16[32,256,512]{2,1,0:T(8,128)(2,1)}, u32[]{:S(2)}, u32[]{:S(2)}) async-start(bf16[32,256,512]{2,1,0:T(8,128)(2,1)} %stack.5), calls=%async_computation | async-start | bytes 16777216 | tf_op jit(solution)/shard_map/all_to_all | solution.py:92
  18.2 1.8 copy.52
  20.2 181.0 %all-to-all-done = bf16[32,256,512]{2,1,0:T(8,128)(2,1)} async-done(((bf16[32,256,512]{2,1,0:T(8,128)(2,1)}), bf16[32,256,512]{2,1,0:T(8,128)(2,1)}, u32[]{:S(2)}, u32[]{:S(2)}) %all-to-all-start) | async-done | bytes 8388640 | tf_op jit(solution)/shard_map/all_to_all | solution.py:92
  201.4 1.6 broadcast.184.clone.1
  203.0 220.7 %while.35 = (s32[]{:T(128)}, bf16[32,8192]{1,0:T(8,128)(2,1)S(1)}, bf16[4,32,8192]{2,1,0:T(8,128)(2,1)S(1)}, bf16[4,32,8192]{2,1,0:T(8,128)(2,1)}, bf16[4,32,64]...) while((s32[]{:T(128)}, bf16[32,8192]{1,0:T(8,128)(2,1)S(1)}, ...), condition=%wide.region_4.5_spmd, body=%wide.region_0.4_spmd.sunk | while | flops 309102624 | bytes 19978252 | solution.py:147
  203.0 4.7 collective-permute-start
  209.0 8.8 %collective-permute-done = bf16[32,8192]{1,0:T(8,128)(2,1)S(1)} collective-permute-done((bf16[32,8192]{1,0:T(8,128)(2,1)S(1)}, bf16[32,8192]{1,0:T(8,128)(2,1)S(1)}, u32[]{:S(2)}, u32[]{:S(2)}) %collective-permute-start) | collective-permute-done | bytes 524320 | tf_op jit(solution)/shard_map/while/body/eval_jaxpr/ppermute | solution.py:37
  219.0 9.1 %conditional.4 = ((bf16[32,8192]{1,0:T(8,128)(2,1)S(1)}, bf16[4,32,8192]{2,1,0:T(8,128)(2,1)S(1)}, bf16[4,32,8192]{2,1,0:T(8,128)(2,1)}, bf16[4,32,64]{2,1,0:T(8,128)(2,1)S(1)})) conditional(s32[]{:T(128)} %convert_element_type.131, (bf16[32,8192]{1,0:T(8,128)(2,1)S(1)}, bf16[4,32,8192]{2,1,0:T(8,128)(2,1)S(1)}, bf16[4,32,8192]{2,1,0:T(8,128)(2,1)}, ...), branch_computations={%region_1.1_spmd, %region_2.3_spmd} | conditional | flops 308840480 | bytes 16307794 | solution.py:136
  219.3 2.1 bitcast_dynamic-update-slice_fusion.2
  221.4 5.0 fusion.6
  230.9 8.3 %collective-permute-done = bf16[32,8192]{1,0:T(8,128)(2,1)S(1)} collective-permute-done((bf16[32,8192]{1,0:T(8,128)(2,1)S(1)}, bf16[32,8192]{1,0:T(8,128)(2,1)S(1)}, u32[]{:S(2)}, u32[]{:S(2)}) %collective-permute-start) | collective-permute-done | bytes 524320 | tf_op jit(solution)/shard_map/while/body/eval_jaxpr/ppermute | solution.py:37
  240.3 9.1 %conditional.4 = ((bf16[32,8192]{1,0:T(8,128)(2,1)S(1)}, bf16[4,32,8192]{2,1,0:T(8,128)(2,1)S(1)}, bf16[4,32,8192]{2,1,0:T(8,128)(2,1)}, bf16[4,32,64]{2,1,0:T(8,128)(2,1)S(1)})) conditional(s32[]{:T(128)} %convert_element_type.131, (bf16[32,8192]{1,0:T(8,128)(2,1)S(1)}, bf16[4,32,8192]{2,1,0:T(8,128)(2,1)S(1)}, bf16[4,32,8192]{2,1,0:T(8,128)(2,1)}, ...), branch_computations={%region_1.1_spmd, %region_2.3_spmd} | conditional | flops 308840480 | bytes 16307794 | solution.py:136
  240.6 2.1 bitcast_dynamic-update-slice_fusion.2
  242.6 5.0 fusion.6
  249.4 5.9 collective-permute-start
  256.7 7.4 collective-permute-done
  265.3 9.1 %conditional.4 = ((bf16[32,8192]{1,0:T(8,128)(2,1)S(1)}, bf16[4,32,8192]{2,1,0:T(8,128)(2,1)S(1)}, bf16[4,32,8192]{2,1,0:T(8,128)(2,1)}, bf16[4,32,64]{2,1,0:T(8,128)(2,1)S(1)})) conditional(s32[]{:T(128)} %convert_element_type.131, (bf16[32,8192]{1,0:T(8,128)(2,1)S(1)}, bf16[4,32,8192]{2,1,0:T(8,128)(2,1)S(1)}, bf16[4,32,8192]{2,1,0:T(8,128)(2,1)}, ...), branch_computations={%region_1.1_spmd, %region_2.3_spmd} | conditional | flops 308840480 | bytes 16307794 | solution.py:136
  265.6 2.1 bitcast_dynamic-update-slice_fusion.2
  267.6 5.0 fusion.6
  274.4 6.0 collective-permute-start
  281.7 6.5 collective-permute-done
  289.4 9.1 %conditional.4 = ((bf16[32,8192]{1,0:T(8,128)(2,1)S(1)}, bf16[4,32,8192]{2,1,0:T(8,128)(2,1)S(1)}, bf16[4,32,8192]{2,1,0:T(8,128)(2,1)}, bf16[4,32,64]{2,1,0:T(8,128)(2,1)S(1)})) conditional(s32[]{:T(128)} %convert_element_type.131, (bf16[32,8192]{1,0:T(8,128)(2,1)S(1)}, bf16[4,32,8192]{2,1,0:T(8,128)(2,1)S(1)}, bf16[4,32,8192]{2,1,0:T(8,128)(2,1)}, ...), branch_computations={%region_1.1_spmd, %region_2.3_spmd} | conditional | flops 308840480 | bytes 16307794 | solution.py:136
  289.7 2.1 bitcast_dynamic-update-slice_fusion.2
  291.8 5.0 fusion.6
  298.5 5.9 collective-permute-start
  305.8 5.7 collective-permute-done
  312.7 15.0 %collective-permute-start = (bf16[32,8192]{1,0:T(8,128)(2,1)S(1)}, bf16[32,8192]{1,0:T(8,128)(2,1)S(1)}, u32[]{:S(2)}, u32[]{:S(2)}) collective-permute-start(bf16[32,8192]{1,0:T(8,128)(2,1)S(1)} %get-tuple-element.647), channel_id=1, source_target_pairs={{0,32},{32,64},{64,96},{96,128},{128,160},{160,192},{192,224},{1,3... | collective-permute-start | bytes 1572872 | tf_op jit(solution)/shard_map/while/body/eval_jaxpr/ppermute | solution.py:37
  329.1 5.3 collective-permute-done
  335.5 5.9 collective-permute-start
  342.8 5.3 collective-permute-done
  349.3 15.5 %collective-permute-start = (bf16[32,8192]{1,0:T(8,128)(2,1)S(1)}, bf16[32,8192]{1,0:T(8,128)(2,1)S(1)}, u32[]{:S(2)}, u32[]{:S(2)}) collective-permute-start(bf16[32,8192]{1,0:T(8,128)(2,1)S(1)} %get-tuple-element.647), channel_id=1, source_target_pairs={{0,32},{32,64},{64,96},{96,128},{128,160},{160,192},{192,224},{1,3... | collective-permute-start | bytes 1572872 | tf_op jit(solution)/shard_map/while/body/eval_jaxpr/ppermute | solution.py:37
  366.2 5.3 collective-permute-done
  372.7 6.8 collective-permute-start
  380.9 5.3 collective-permute-done
  387.4 12.4 %collective-permute-start = (bf16[32,8192]{1,0:T(8,128)(2,1)S(1)}, bf16[32,8192]{1,0:T(8,128)(2,1)S(1)}, u32[]{:S(2)}, u32[]{:S(2)}) collective-permute-start(bf16[32,8192]{1,0:T(8,128)(2,1)S(1)} %get-tuple-element.647), channel_id=1, source_target_pairs={{0,32},{32,64},{64,96},{96,128},{128,160},{160,192},{192,224},{1,3... | collective-permute-start | bytes 1572872 | tf_op jit(solution)/shard_map/while/body/eval_jaxpr/ppermute | solution.py:37
  401.1 7.6 %collective-permute-done = bf16[32,8192]{1,0:T(8,128)(2,1)S(1)} collective-permute-done((bf16[32,8192]{1,0:T(8,128)(2,1)S(1)}, bf16[32,8192]{1,0:T(8,128)(2,1)S(1)}, u32[]{:S(2)}, u32[]{:S(2)}) %collective-permute-start) | collective-permute-done | bytes 524320 | tf_op jit(solution)/shard_map/while/body/eval_jaxpr/ppermute | solution.py:37
  409.9 5.9 collective-permute-start
  417.2 5.3 collective-permute-done
  425.3 279.7 %while.36 = (s32[]{:T(128)}, bf16[32,8192]{1,0:T(8,128)(2,1)S(1)}, bf16[4,32,8192]{2,1,0:T(8,128)(2,1)}, bf16[4,32,512]{2,1,0:T(8,128)(2,1)S(1)}, bf16[4,32,64]{...) while((s32[]{:T(128)}, bf16[32,8192]{1,0:T(8,128)(2,1)S(1)}, ...), condition=%wide.region_11.12_spmd, body=%wide.region_5.11_spmd.sunk | while | flops 309186592 | bytes 28268232 | solution.py:204
  427.9 22.3 %collective-permute-done.1 = bf16[32,8192]{1,0:T(8,128)(2,1)S(1)} collective-permute-done((bf16[32,8192]{1,0:T(8,128)(2,1)S(1)}, bf16[32,8192]{1,0:T(8,128)(2,1)S(1)}, u32[]{:S(2)}, u32[]{:S(2)}) %collective-permute-start.1) | collective-permute-done | bytes 524320 | tf_op jit(solution)/shard_map/while/body/eval_jaxpr/ppermute | solution.py:37
  453.9 12.2 %collective-permute-done.1 = bf16[32,8192]{1,0:T(8,128)(2,1)S(1)} collective-permute-done((bf16[32,8192]{1,0:T(8,128)(2,1)S(1)}, bf16[32,8192]{1,0:T(8,128)(2,1)S(1)}, u32[]{:S(2)}, u32[]{:S(2)}) %collective-permute-start.1) | collective-permute-done | bytes 524320 | tf_op jit(solution)/shard_map/while/body/eval_jaxpr/ppermute | solution.py:37
  469.9 20.3 %collective-permute-done.1 = bf16[32,8192]{1,0:T(8,128)(2,1)S(1)} collective-permute-done((bf16[32,8192]{1,0:T(8,128)(2,1)S(1)}, bf16[32,8192]{1,0:T(8,128)(2,1)S(1)}, u32[]{:S(2)}, u32[]{:S(2)}) %collective-permute-start.1) | collective-permute-done | bytes 524320 | tf_op jit(solution)/shard_map/while/body/eval_jaxpr/ppermute | solution.py:37
  494.0 16.3 %collective-permute-done.1 = bf16[32,8192]{1,0:T(8,128)(2,1)S(1)} collective-permute-done((bf16[32,8192]{1,0:T(8,128)(2,1)S(1)}, bf16[32,8192]{1,0:T(8,128)(2,1)S(1)}, u32[]{:S(2)}, u32[]{:S(2)}) %collective-permute-start.1) | collective-permute-done | bytes 524320 | tf_op jit(solution)/shard_map/while/body/eval_jaxpr/ppermute | solution.py:37
  514.1 22.8 %collective-permute-done.1 = bf16[32,8192]{1,0:T(8,128)(2,1)S(1)} collective-permute-done((bf16[32,8192]{1,0:T(8,128)(2,1)S(1)}, bf16[32,8192]{1,0:T(8,128)(2,1)S(1)}, u32[]{:S(2)}, u32[]{:S(2)}) %collective-permute-start.1) | collective-permute-done | bytes 524320 | tf_op jit(solution)/shard_map/while/body/eval_jaxpr/ppermute | solution.py:37
  540.6 15.7 %collective-permute-done.1 = bf16[32,8192]{1,0:T(8,128)(2,1)S(1)} collective-permute-done((bf16[32,8192]{1,0:T(8,128)(2,1)S(1)}, bf16[32,8192]{1,0:T(8,128)(2,1)S(1)}, u32[]{:S(2)}, u32[]{:S(2)}) %collective-permute-start.1) | collective-permute-done | bytes 524320 | tf_op jit(solution)/shard_map/while/body/eval_jaxpr/ppermute | solution.py:37
  560.1 10.0 %collective-permute-done.1 = bf16[32,8192]{1,0:T(8,128)(2,1)S(1)} collective-permute-done((bf16[32,8192]{1,0:T(8,128)(2,1)S(1)}, bf16[32,8192]{1,0:T(8,128)(2,1)S(1)}, u32[]{:S(2)}, u32[]{:S(2)}) %collective-permute-start.1) | collective-permute-done | bytes 524320 | tf_op jit(solution)/shard_map/while/body/eval_jaxpr/ppermute | solution.py:37
  573.9 40.0 %collective-permute-done.1 = bf16[32,8192]{1,0:T(8,128)(2,1)S(1)} collective-permute-done((bf16[32,8192]{1,0:T(8,128)(2,1)S(1)}, bf16[32,8192]{1,0:T(8,128)(2,1)S(1)}, u32[]{:S(2)}, u32[]{:S(2)}) %collective-permute-start.1) | collective-permute-done | bytes 524320 | tf_op jit(solution)/shard_map/while/body/eval_jaxpr/ppermute | solution.py:37
  615.1 8.8 %conditional.5 = ((bf16[32,8192]{1,0:T(8,128)(2,1)S(1)}, bf16[4,32,8192]{2,1,0:T(8,128)(2,1)}, bf16[4,32,512]{2,1,0:T(8,128)(2,1)S(1)}, bf16[4,32,64]{2,1,0:T(8,128)(2,1)S(1)})) conditional(s32[]{:T(128)} %convert_element_type.132, (bf16[32,8192]{1,0:T(8,128)(2,1)S(1)}, bf16[4,32,8192]{2,1,0:T(8,128)(2,1)}, bf16[4,32,512]{2,1,0:T(8,128)(2,1)S(1)}, ...), branch_computations={%region_6.6_spmd, %region_7.10_spmd} | conditional | flops 308924448 | bytes 24597758 | solution.py:190
  615.7 6.1 fusion.12
  626.5 12.4 %collective-permute-done.1 = bf16[32,8192]{1,0:T(8,128)(2,1)S(1)} collective-permute-done((bf16[32,8192]{1,0:T(8,128)(2,1)S(1)}, bf16[32,8192]{1,0:T(8,128)(2,1)S(1)}, u32[]{:S(2)}, u32[]{:S(2)}) %collective-permute-start.1) | collective-permute-done | bytes 524320 | tf_op jit(solution)/shard_map/while/body/eval_jaxpr/ppermute | solution.py:37
  640.1 8.8 %conditional.5 = ((bf16[32,8192]{1,0:T(8,128)(2,1)S(1)}, bf16[4,32,8192]{2,1,0:T(8,128)(2,1)}, bf16[4,32,512]{2,1,0:T(8,128)(2,1)S(1)}, bf16[4,32,64]{2,1,0:T(8,128)(2,1)S(1)})) conditional(s32[]{:T(128)} %convert_element_type.132, (bf16[32,8192]{1,0:T(8,128)(2,1)S(1)}, bf16[4,32,8192]{2,1,0:T(8,128)(2,1)}, bf16[4,32,512]{2,1,0:T(8,128)(2,1)S(1)}, ...), branch_computations={%region_6.6_spmd, %region_7.10_spmd} | conditional | flops 308924448 | bytes 24597758 | solution.py:190
  640.7 6.1 fusion.12
  651.5 13.8 %collective-permute-done.1 = bf16[32,8192]{1,0:T(8,128)(2,1)S(1)} collective-permute-done((bf16[32,8192]{1,0:T(8,128)(2,1)S(1)}, bf16[32,8192]{1,0:T(8,128)(2,1)S(1)}, u32[]{:S(2)}, u32[]{:S(2)}) %collective-permute-start.1) | collective-permute-done | bytes 524320 | tf_op jit(solution)/shard_map/while/body/eval_jaxpr/ppermute | solution.py:37
  666.5 8.8 %conditional.5 = ((bf16[32,8192]{1,0:T(8,128)(2,1)S(1)}, bf16[4,32,8192]{2,1,0:T(8,128)(2,1)}, bf16[4,32,512]{2,1,0:T(8,128)(2,1)S(1)}, bf16[4,32,64]{2,1,0:T(8,128)(2,1)S(1)})) conditional(s32[]{:T(128)} %convert_element_type.132, (bf16[32,8192]{1,0:T(8,128)(2,1)S(1)}, bf16[4,32,8192]{2,1,0:T(8,128)(2,1)}, bf16[4,32,512]{2,1,0:T(8,128)(2,1)S(1)}, ...), branch_computations={%region_6.6_spmd, %region_7.10_spmd} | conditional | flops 308924448 | bytes 24597758 | solution.py:190
  667.1 6.1 fusion.12
  677.9 17.2 %collective-permute-done.1 = bf16[32,8192]{1,0:T(8,128)(2,1)S(1)} collective-permute-done((bf16[32,8192]{1,0:T(8,128)(2,1)S(1)}, bf16[32,8192]{1,0:T(8,128)(2,1)S(1)}, u32[]{:S(2)}, u32[]{:S(2)}) %collective-permute-start.1) | collective-permute-done | bytes 524320 | tf_op jit(solution)/shard_map/while/body/eval_jaxpr/ppermute | solution.py:37
  696.2 8.8 %conditional.5 = ((bf16[32,8192]{1,0:T(8,128)(2,1)S(1)}, bf16[4,32,8192]{2,1,0:T(8,128)(2,1)}, bf16[4,32,512]{2,1,0:T(8,128)(2,1)S(1)}, bf16[4,32,64]{2,1,0:T(8,128)(2,1)S(1)})) conditional(s32[]{:T(128)} %convert_element_type.132, (bf16[32,8192]{1,0:T(8,128)(2,1)S(1)}, bf16[4,32,8192]{2,1,0:T(8,128)(2,1)}, bf16[4,32,512]{2,1,0:T(8,128)(2,1)S(1)}, ...), branch_computations={%region_6.6_spmd, %region_7.10_spmd} | conditional | flops 308924448 | bytes 24597758 | solution.py:190
  696.8 6.1 fusion.12
  706.1 9.7 %all-to-all-start.2 = ((bf16[32,2,512]{2,1,0:T(2,128)(2,1)}), bf16[32,2,512]{2,1,0:T(2,128)(2,1)S(1)}, u32[]{:S(2)}, u32[]{:S(2)}) async-start(bf16[32,2,512]{2,1,0:T(2,128)(2,1)} %reshape.113), calls=%async_computation.2 | async-start | bytes 131072 | tf_op jit(solution)/shard_map/all_to_all | solution.py:48
  715.9 2.1 fusion.16
  719.1 4.8 all-to-all-done.2
  723.9 5.0 all-to-all-start.1
  729.7 28.3 %all-to-all-done.1 = bf16[32,256,64]{1,2,0:T(8,128)(2,1)S(1)} async-done(((bf16[32,256,64]{1,2,0:T(8,128)(2,1)}), bf16[32,256,64]{1,2,0:T(8,128)(2,1)S(1)}, u32[]{:S(2)}, u32[]{:S(2)}) %all-to-all-start.1) | async-done | bytes 1048608 | tf_op jit(solution)/shard_map/all_to_all | solution.py:48
  (188 shorter events, 82.9 us)
Async XLA Ops:
  8.3 9.9 %copy-start.1 = (bf16[1,8192,64]{1,2,0:T(8,128)(2,1)S(1)}, bf16[1,8192,64]{1,2,0:T(8,128)(2,1)}, u32[]{:S(2)}) copy-start(bf16[1,8192,64]{1,2,0:T(8,128)(2,1)} %param.20) | copy-start | bytes 3145732
  8.3 192.9 %all-to-all-start = ((bf16[32,256,512]{2,1,0:T(8,128)(2,1)}), bf16[32,256,512]{2,1,0:T(8,128)(2,1)}, u32[]{:S(2)}, u32[]{:S(2)}) async-start(bf16[32,256,512]{2,1,0:T(8,128)(2,1)} %stack.5), calls=%async_computation | async-start | bytes 16777216 | tf_op jit(solution)/shard_map/all_to_all | solution.py:92
  18.1 1.9 copy-start.2
  18.1 2.0 copy-start.3
  203.0 14.9 %collective-permute-start = (bf16[32,8192]{1,0:T(8,128)(2,1)S(1)}, bf16[32,8192]{1,0:T(8,128)(2,1)S(1)}, u32[]{:S(2)}, u32[]{:S(2)}) collective-permute-start(bf16[32,8192]{1,0:T(8,128)(2,1)S(1)} %get-tuple-element.647), channel_id=1, source_target_pairs={{0,32},{32,64},{64,96},{96,128},{128,160},{160,192},{192,224},{1,3... | collective-permute-start | bytes 1572872 | tf_op jit(solution)/shard_map/while/body/eval_jaxpr/ppermute | solution.py:37
  228.2 11.0 %collective-permute-start = (bf16[32,8192]{1,0:T(8,128)(2,1)S(1)}, bf16[32,8192]{1,0:T(8,128)(2,1)S(1)}, u32[]{:S(2)}, u32[]{:S(2)}) collective-permute-start(bf16[32,8192]{1,0:T(8,128)(2,1)S(1)} %get-tuple-element.647), channel_id=1, source_target_pairs={{0,32},{32,64},{64,96},{96,128},{128,160},{160,192},{192,224},{1,3... | collective-permute-start | bytes 1572872 | tf_op jit(solution)/shard_map/while/body/eval_jaxpr/ppermute | solution.py:37
  249.4 14.7 %collective-permute-start = (bf16[32,8192]{1,0:T(8,128)(2,1)S(1)}, bf16[32,8192]{1,0:T(8,128)(2,1)S(1)}, u32[]{:S(2)}, u32[]{:S(2)}) collective-permute-start(bf16[32,8192]{1,0:T(8,128)(2,1)S(1)} %get-tuple-element.647), channel_id=1, source_target_pairs={{0,32},{32,64},{64,96},{96,128},{128,160},{160,192},{192,224},{1,3... | collective-permute-start | bytes 1572872 | tf_op jit(solution)/shard_map/while/body/eval_jaxpr/ppermute | solution.py:37
  274.4 13.9 %collective-permute-start = (bf16[32,8192]{1,0:T(8,128)(2,1)S(1)}, bf16[32,8192]{1,0:T(8,128)(2,1)S(1)}, u32[]{:S(2)}, u32[]{:S(2)}) collective-permute-start(bf16[32,8192]{1,0:T(8,128)(2,1)S(1)} %get-tuple-element.647), channel_id=1, source_target_pairs={{0,32},{32,64},{64,96},{96,128},{128,160},{160,192},{192,224},{1,3... | collective-permute-start | bytes 1572872 | tf_op jit(solution)/shard_map/while/body/eval_jaxpr/ppermute | solution.py:37
  298.5 13.0 %collective-permute-start = (bf16[32,8192]{1,0:T(8,128)(2,1)S(1)}, bf16[32,8192]{1,0:T(8,128)(2,1)S(1)}, u32[]{:S(2)}, u32[]{:S(2)}) collective-permute-start(bf16[32,8192]{1,0:T(8,128)(2,1)S(1)} %get-tuple-element.647), channel_id=1, source_target_pairs={{0,32},{32,64},{64,96},{96,128},{128,160},{160,192},{192,224},{1,3... | collective-permute-start | bytes 1572872 | tf_op jit(solution)/shard_map/while/body/eval_jaxpr/ppermute | solution.py:37
  312.7 21.6 %collective-permute-start = (bf16[32,8192]{1,0:T(8,128)(2,1)S(1)}, bf16[32,8192]{1,0:T(8,128)(2,1)S(1)}, u32[]{:S(2)}, u32[]{:S(2)}) collective-permute-start(bf16[32,8192]{1,0:T(8,128)(2,1)S(1)} %get-tuple-element.647), channel_id=1, source_target_pairs={{0,32},{32,64},{64,96},{96,128},{128,160},{160,192},{192,224},{1,3... | collective-permute-start | bytes 1572872 | tf_op jit(solution)/shard_map/while/body/eval_jaxpr/ppermute | solution.py:37
  335.5 12.6 %collective-permute-start = (bf16[32,8192]{1,0:T(8,128)(2,1)S(1)}, bf16[32,8192]{1,0:T(8,128)(2,1)S(1)}, u32[]{:S(2)}, u32[]{:S(2)}) collective-permute-start(bf16[32,8192]{1,0:T(8,128)(2,1)S(1)} %get-tuple-element.647), channel_id=1, source_target_pairs={{0,32},{32,64},{64,96},{96,128},{128,160},{160,192},{192,224},{1,3... | collective-permute-start | bytes 1572872 | tf_op jit(solution)/shard_map/while/body/eval_jaxpr/ppermute | solution.py:37
  349.3 22.1 %collective-permute-start = (bf16[32,8192]{1,0:T(8,128)(2,1)S(1)}, bf16[32,8192]{1,0:T(8,128)(2,1)S(1)}, u32[]{:S(2)}, u32[]{:S(2)}) collective-permute-start(bf16[32,8192]{1,0:T(8,128)(2,1)S(1)} %get-tuple-element.647), channel_id=1, source_target_pairs={{0,32},{32,64},{64,96},{96,128},{128,160},{160,192},{192,224},{1,3... | collective-permute-start | bytes 1572872 | tf_op jit(solution)/shard_map/while/body/eval_jaxpr/ppermute | solution.py:37
  372.7 13.5 %collective-permute-start = (bf16[32,8192]{1,0:T(8,128)(2,1)S(1)}, bf16[32,8192]{1,0:T(8,128)(2,1)S(1)}, u32[]{:S(2)}, u32[]{:S(2)}) collective-permute-start(bf16[32,8192]{1,0:T(8,128)(2,1)S(1)} %get-tuple-element.647), channel_id=1, source_target_pairs={{0,32},{32,64},{64,96},{96,128},{128,160},{160,192},{192,224},{1,3... | collective-permute-start | bytes 1572872 | tf_op jit(solution)/shard_map/while/body/eval_jaxpr/ppermute | solution.py:37
  387.4 21.4 %collective-permute-start = (bf16[32,8192]{1,0:T(8,128)(2,1)S(1)}, bf16[32,8192]{1,0:T(8,128)(2,1)S(1)}, u32[]{:S(2)}, u32[]{:S(2)}) collective-permute-start(bf16[32,8192]{1,0:T(8,128)(2,1)S(1)} %get-tuple-element.647), channel_id=1, source_target_pairs={{0,32},{32,64},{64,96},{96,128},{128,160},{160,192},{192,224},{1,3... | collective-permute-start | bytes 1572872 | tf_op jit(solution)/shard_map/while/body/eval_jaxpr/ppermute | solution.py:37
  409.9 12.6 %collective-permute-start = (bf16[32,8192]{1,0:T(8,128)(2,1)S(1)}, bf16[32,8192]{1,0:T(8,128)(2,1)S(1)}, u32[]{:S(2)}, u32[]{:S(2)}) collective-permute-start(bf16[32,8192]{1,0:T(8,128)(2,1)S(1)} %get-tuple-element.647), channel_id=1, source_target_pairs={{0,32},{32,64},{64,96},{96,128},{128,160},{160,192},{192,224},{1,3... | collective-permute-start | bytes 1572872 | tf_op jit(solution)/shard_map/while/body/eval_jaxpr/ppermute | solution.py:37
  425.3 24.8 %collective-permute-start.1 = (bf16[32,8192]{1,0:T(8,128)(2,1)S(1)}, bf16[32,8192]{1,0:T(8,128)(2,1)S(1)}, u32[]{:S(2)}, u32[]{:S(2)}) collective-permute-start(bf16[32,8192]{1,0:T(8,128)(2,1)S(1)} %get-tuple-element.705), channel_id=1, source_target_pairs={{32,0},{64,32},{96,64},{128,96},{160,128},{192,160},{224,192},{33,... | collective-permute-start | bytes 1572872 | tf_op jit(solution)/shard_map/while/body/eval_jaxpr/ppermute | solution.py:37
  451.4 14.8 %collective-permute-start.1 = (bf16[32,8192]{1,0:T(8,128)(2,1)S(1)}, bf16[32,8192]{1,0:T(8,128)(2,1)S(1)}, u32[]{:S(2)}, u32[]{:S(2)}) collective-permute-start(bf16[32,8192]{1,0:T(8,128)(2,1)S(1)} %get-tuple-element.705), channel_id=1, source_target_pairs={{32,0},{64,32},{96,64},{128,96},{160,128},{192,160},{224,192},{33,... | collective-permute-start | bytes 1572872 | tf_op jit(solution)/shard_map/while/body/eval_jaxpr/ppermute | solution.py:37
  467.4 22.9 %collective-permute-start.1 = (bf16[32,8192]{1,0:T(8,128)(2,1)S(1)}, bf16[32,8192]{1,0:T(8,128)(2,1)S(1)}, u32[]{:S(2)}, u32[]{:S(2)}) collective-permute-start(bf16[32,8192]{1,0:T(8,128)(2,1)S(1)} %get-tuple-element.705), channel_id=1, source_target_pairs={{32,0},{64,32},{96,64},{128,96},{160,128},{192,160},{224,192},{33,... | collective-permute-start | bytes 1572872 | tf_op jit(solution)/shard_map/while/body/eval_jaxpr/ppermute | solution.py:37
  491.4 18.8 %collective-permute-start.1 = (bf16[32,8192]{1,0:T(8,128)(2,1)S(1)}, bf16[32,8192]{1,0:T(8,128)(2,1)S(1)}, u32[]{:S(2)}, u32[]{:S(2)}) collective-permute-start(bf16[32,8192]{1,0:T(8,128)(2,1)S(1)} %get-tuple-element.705), channel_id=1, source_target_pairs={{32,0},{64,32},{96,64},{128,96},{160,128},{192,160},{224,192},{33,... | collective-permute-start | bytes 1572872 | tf_op jit(solution)/shard_map/while/body/eval_jaxpr/ppermute | solution.py:37
  511.5 25.3 %collective-permute-start.1 = (bf16[32,8192]{1,0:T(8,128)(2,1)S(1)}, bf16[32,8192]{1,0:T(8,128)(2,1)S(1)}, u32[]{:S(2)}, u32[]{:S(2)}) collective-permute-start(bf16[32,8192]{1,0:T(8,128)(2,1)S(1)} %get-tuple-element.705), channel_id=1, source_target_pairs={{32,0},{64,32},{96,64},{128,96},{160,128},{192,160},{224,192},{33,... | collective-permute-start | bytes 1572872 | tf_op jit(solution)/shard_map/while/body/eval_jaxpr/ppermute | solution.py:37
  538.0 18.3 %collective-permute-start.1 = (bf16[32,8192]{1,0:T(8,128)(2,1)S(1)}, bf16[32,8192]{1,0:T(8,128)(2,1)S(1)}, u32[]{:S(2)}, u32[]{:S(2)}) collective-permute-start(bf16[32,8192]{1,0:T(8,128)(2,1)S(1)} %get-tuple-element.705), channel_id=1, source_target_pairs={{32,0},{64,32},{96,64},{128,96},{160,128},{192,160},{224,192},{33,... | collective-permute-start | bytes 1572872 | tf_op jit(solution)/shard_map/while/body/eval_jaxpr/ppermute | solution.py:37
  557.5 12.6 %collective-permute-start.1 = (bf16[32,8192]{1,0:T(8,128)(2,1)S(1)}, bf16[32,8192]{1,0:T(8,128)(2,1)S(1)}, u32[]{:S(2)}, u32[]{:S(2)}) collective-permute-start(bf16[32,8192]{1,0:T(8,128)(2,1)S(1)} %get-tuple-element.705), channel_id=1, source_target_pairs={{32,0},{64,32},{96,64},{128,96},{160,128},{192,160},{224,192},{33,... | collective-permute-start | bytes 1572872 | tf_op jit(solution)/shard_map/while/body/eval_jaxpr/ppermute | solution.py:37
  571.3 42.6 %collective-permute-start.1 = (bf16[32,8192]{1,0:T(8,128)(2,1)S(1)}, bf16[32,8192]{1,0:T(8,128)(2,1)S(1)}, u32[]{:S(2)}, u32[]{:S(2)}) collective-permute-start(bf16[32,8192]{1,0:T(8,128)(2,1)S(1)} %get-tuple-element.705), channel_id=1, source_target_pairs={{32,0},{64,32},{96,64},{128,96},{160,128},{192,160},{224,192},{33,... | collective-permute-start | bytes 1572872 | tf_op jit(solution)/shard_map/while/body/eval_jaxpr/ppermute | solution.py:37
  615.7 6.1 copy-start
  623.9 15.0 %collective-permute-start.1 = (bf16[32,8192]{1,0:T(8,128)(2,1)S(1)}, bf16[32,8192]{1,0:T(8,128)(2,1)S(1)}, u32[]{:S(2)}, u32[]{:S(2)}) collective-permute-start(bf16[32,8192]{1,0:T(8,128)(2,1)S(1)} %get-tuple-element.705), channel_id=1, source_target_pairs={{32,0},{64,32},{96,64},{128,96},{160,128},{192,160},{224,192},{33,... | collective-permute-start | bytes 1572872 | tf_op jit(solution)/shard_map/while/body/eval_jaxpr/ppermute | solution.py:37
  640.7 6.1 copy-start
  648.9 16.4 %collective-permute-start.1 = (bf16[32,8192]{1,0:T(8,128)(2,1)S(1)}, bf16[32,8192]{1,0:T(8,128)(2,1)S(1)}, u32[]{:S(2)}, u32[]{:S(2)}) collective-permute-start(bf16[32,8192]{1,0:T(8,128)(2,1)S(1)} %get-tuple-element.705), channel_id=1, source_target_pairs={{32,0},{64,32},{96,64},{128,96},{160,128},{192,160},{224,192},{33,... | collective-permute-start | bytes 1572872 | tf_op jit(solution)/shard_map/while/body/eval_jaxpr/ppermute | solution.py:37
  667.1 6.1 copy-start
  675.3 19.7 %collective-permute-start.1 = (bf16[32,8192]{1,0:T(8,128)(2,1)S(1)}, bf16[32,8192]{1,0:T(8,128)(2,1)S(1)}, u32[]{:S(2)}, u32[]{:S(2)}) collective-permute-start(bf16[32,8192]{1,0:T(8,128)(2,1)S(1)} %get-tuple-element.705), channel_id=1, source_target_pairs={{32,0},{64,32},{96,64},{128,96},{160,128},{192,160},{224,192},{33,... | collective-permute-start | bytes 1572872 | tf_op jit(solution)/shard_map/while/body/eval_jaxpr/ppermute | solution.py:37
  696.8 6.1 copy-start
  706.1 17.8 %all-to-all-start.2 = ((bf16[32,2,512]{2,1,0:T(2,128)(2,1)}), bf16[32,2,512]{2,1,0:T(2,128)(2,1)S(1)}, u32[]{:S(2)}, u32[]{:S(2)}) async-start(bf16[32,2,512]{2,1,0:T(2,128)(2,1)} %reshape.113), calls=%async_computation.2 | async-start | bytes 131072 | tf_op jit(solution)/shard_map/all_to_all | solution.py:48
  723.9 34.0 %all-to-all-start.1 = ((bf16[32,256,64]{1,2,0:T(8,128)(2,1)}), bf16[32,256,64]{1,2,0:T(8,128)(2,1)S(1)}, u32[]{:S(2)}, u32[]{:S(2)}) async-start(bf16[32,256,64]{1,2,0:T(8,128)(2,1)} %bitcast.80), calls=%async_computation.1 | async-start | bytes 2097152 | tf_op jit(solution)/shard_map/all_to_all | solution.py:48
